TPU v7x, 32 devices: a whole 2x2x4 slice. The times are simulated.
32 devices in a mesh: groups: 2 (over y), ep: 16 (over z, x, core).
Axes of the slice: x: 2, y: 2, z: 4, core: 2. Of those that a mesh axis runs over, the one named last changes fastest.
Arguments:
- tokens: bfloat16 [512, 2880], P(('groups', 'ep')), parts along dimension 0, may hold values from -6 to 6
- routes: int32 [512, 4], P(('groups', 'ep')), parts along dimension 0, may hold values from 0 to 7, all different within a row; in each aligned block of 16 rows (0 to 15, 16 to 31, ...) at most 16 rows name the same one
- gate_fixed: int32 [512, 4], P(('groups', 'ep')), parts along dimension 0, may hold values from 1 to 65535
- gate_weight: bfloat16 [16, 2880, 720], P('ep'), may hold values from -0.109375 to 0.109375
- up_weight: bfloat16 [16, 2880, 720], P('ep'), may hold values from -0.109375 to 0.109375
- down_weight: bfloat16 [16, 720, 2880], P('ep'), may hold values from -0.15625 to 0.15625
Outputs:
- mixed: bfloat16 [512, 2880], P(('groups', 'ep')), parts along dimension 0
There are 2 independent parts, one for each index of `groups`. A program takes and returns all parts, laid end to end along the dimension named above; an argument that names none is the same for every part. Nothing has to cross between parts.
Inputs may be any that keep to these rules, and one draw needn't show every extreme that they name: `routes`: each row names 4 different experts; the 16 rows of one device name any one expert at most 16 times.
All inputs are finite; a program needn't handle non-finite values.
Results may differ from a plain program's by a relative error of at most 0.0065.
Values may be sent and summed in bfloat16 or wider, within the bound.
A program may use at most 64 MiB of HBM per device.

v0:
```python
import functools

import jax
import jax.numpy as jnp
from jax import lax
from jax.experimental import pallas as pl
from jax.experimental.pallas import tpu as pltpu
from jax.sharding import PartitionSpec as P


def swapped(value, axis, bit):
    mask = 2**bit
    pairs = [(source, source ^ mask) for source in range(lax.axis_size(axis))]
    return lax.ppermute(value, axis, pairs)


def expert_half(expert_rows, w_gate, w_up, w_down):
    gate_part = jnp.dot(expert_rows, w_gate, preferred_element_type=jnp.float32)
    up_part = jnp.dot(expert_rows, w_up, preferred_element_type=jnp.float32)
    hidden = (jax.nn.silu(gate_part) * up_part).astype(jnp.bfloat16)
    return jnp.dot(hidden, w_down, preferred_element_type=jnp.float32).astype(jnp.bfloat16)


def local(tokens, routes, gate_fixed, gate_weight, up_weight, down_weight):
    devices_ep = lax.axis_size("ep")
    experts = devices_ep // 2
    tok_count = tokens.shape[0]
    top_count = routes.shape[1]
    width = tokens.shape[1]
    capacity = 2 * tok_count * top_count // experts
    onehot = (routes[:, :, None] == jnp.arange(experts, dtype=jnp.int32)).astype(jnp.int32)
    flat_hot = onehot.reshape(tok_count * top_count, experts)
    before = jnp.cumsum(flat_hot, axis=0) - flat_hot
    position = jnp.sum(before * flat_hot, axis=1).reshape(tok_count, top_count)
    slot_index = routes * capacity + position
    select = (slot_index[:, :, None] == jnp.arange(experts * capacity, dtype=jnp.int32)).astype(
        jnp.int32
    )
    select = jnp.sum(select, axis=1).astype(jnp.bfloat16)
    packed = jnp.einsum("ts,td->sd", select, tokens, preferred_element_type=jnp.float32).astype(
        jnp.bfloat16
    )
    packed = packed.reshape(experts, 1, capacity, width)
    outgoing = jnp.broadcast_to(packed, (experts, 2, capacity, width)).reshape(
        devices_ep, capacity, width
    )
    received = lax.all_to_all(outgoing, "ep", split_axis=0, concat_axis=0, tiled=True)
    result = expert_half(received.reshape(-1, width), gate_weight[0], up_weight[0], down_weight[0])
    partial_value = result.reshape(received.shape[0], received.shape[1], width)
    parity = lax.axis_index("ep") % 2
    halves = partial_value.reshape(devices_ep, capacity, 2, width // 2)
    kept_half = lax.dynamic_index_in_dim(halves, parity, 2, keepdims=False)
    given_half = lax.dynamic_index_in_dim(halves, 1 - parity, 2, keepdims=False)
    partner = swapped(given_half, "ep", 0)
    reduced = (kept_half.astype(jnp.float32) + partner.astype(jnp.float32)).astype(jnp.bfloat16)
    returned = lax.all_to_all(reduced, "ep", split_axis=0, concat_axis=0, tiled=True)
    ordered = returned.reshape(experts, 2, capacity, width // 2).transpose(0, 2, 1, 3)
    expert_out = ordered.reshape(experts * capacity, width)
    picked = jnp.take(expert_out, slot_index.reshape(-1), axis=0).reshape(
        tok_count, top_count, width
    )
    weights = gate_fixed.astype(jnp.float32) / 65536.0
    mixed = jnp.sum(weights[:, :, None] * picked.astype(jnp.float32), axis=1)
    return mixed.astype(jnp.bfloat16)


NT = (((1,), (1,)), ((), ()))


def column_cuts(width, step):
    return [(low, min(low + step, width)) for low in range(0, width, step)]


def dense_kernel(
    slow, fast, tokens, routes, gates, w_gate, w_up, w_down, out,
    gathered, vm_gate, vm_up, vm_down, partial, from_core, to_fast, from_fast, to_slow, from_slow,
    w_sem, ag_send, ag_recv, core_send, core_recv, fast_send, fast_recv, slow_send, slow_recv,
    pass_send, pass_recv, give_send, give_recv,
):
    rows, width = tokens.shape
    top = routes.shape[0]
    padded = gathered.shape[1]
    hidden_count = vm_gate.shape[0]
    device = lax.axis_index("ep")
    core = lax.rem(device, 2)
    chip = device // 2
    at_slow = chip // fast
    at_fast = lax.rem(chip, fast)

    weights = [
        pltpu.make_async_copy(source.at[0], target, w_sem.at[i])
        for i, (source, target) in enumerate(((w_gate, vm_gate), (w_up, vm_up), (w_down, vm_down)))
    ]
    for copy in weights:
        copy.start()

    def name(s, f, c):
        return {"ep": (s * fast + f) * 2 + c}

    def slow_at(off):
        return lax.rem(at_slow + off, slow)

    def fast_at(off):
        return lax.rem(at_fast + off, fast)

    def block(s, f, c):
        start = ((s * 2 + c) * fast + f) * rows
        return pl.ds(pl.multiple_of(start, rows), rows)

    def send(source, target, send_sem, recv_sem, device_id):
        return pltpu.make_async_remote_copy(
            src_ref=source, dst_ref=target, send_sem=send_sem, recv_sem=recv_sem,
            device_id=device_id, device_id_type=pl.DeviceIdType.MESH,
        )

    peers = [name(slow_at(off), at_fast, core) for off in range(1, slow)]
    peers += [name(at_slow, fast_at(off), core) for off in range(1, fast)]
    peers += [name(at_slow, at_fast, 1 - core)]
    barrier = pltpu.get_barrier_semaphore()
    for peer in peers:
        pl.semaphore_signal(barrier, inc=1, device_id=peer, device_id_type=pl.DeviceIdType.MESH)

    mine = block(at_slow, at_fast, core)
    edge = width // 128 * 128
    lanes = lax.broadcasted_iota(jnp.int32, (rows, padded - edge), 1) + edge
    gathered[mine, edge:] = jnp.zeros((rows, padded - edge), jnp.bfloat16)
    gathered[mine, :width] = tokens[...]
    scale = jnp.transpose(gates[...].astype(jnp.float32)) / 65536.0
    high = scale.astype(jnp.bfloat16).astype(jnp.float32)
    low = scale - high
    ids = jnp.transpose(routes[...].astype(jnp.float32))
    tail = gathered[mine, edge:].astype(jnp.float32)
    for k in range(top):
        tail = jnp.where(lanes == width + k, ids[:, k : k + 1], tail)
        tail = jnp.where(lanes == width + top + k, high[:, k : k + 1], tail)
        tail = jnp.where(lanes == width + 2 * top + k, low[:, k : k + 1], tail)
    gathered[mine, edge:] = tail.astype(jnp.bfloat16)

    pl.semaphore_wait(barrier, len(peers))

    started = []

    def launch(copy):
        copy.start()
        started.append(copy)

    def to_partner(s, f, slot):
        where = gathered.at[block(s, f, core)]
        launch(send(where, where, core_send.at[slot], core_recv.at[slot], name(at_slow, at_fast, 1 - core)))

    def along_fast(s, step):
        where = gathered.at[block(s, at_fast, core)]
        for off in range(1, fast):
            launch(send(where, where, fast_send.at[step, off], fast_recv.at[step, off], name(at_slow, fast_at(off), core)))

    here = gathered.at[mine]
    along_fast(at_slow, slow - 1)
    outward, across = at_slow + 1 - 2 * lax.rem(at_slow, 2), slow - 1 - at_slow
    inner = (at_slow % 3) != 0

    def to_slow_chip(s, place, sem, slot):
        where = gathered.at[block(s, at_fast, core)]
        return send(where, where, ag_send.at[sem], ag_recv.at[slot], name(place, at_fast, core))

    to_slow_chip(at_slow, outward, 0, 0).start()

    @pl.when(inner)
    def _():
        to_slow_chip(at_slow, across, 1, 1).start()

    to_partner(at_slow, at_fast, (slow - 1) * fast)

    own = slow - 1
    order = [own] + list(range(own))
    chunk_rows = 2 * fast * rows

    def source(step):
        return [outward, 2 - at_slow // 2, 3 - 3 * (at_slow // 2), at_slow][step]

    def take_slow(step):
        if step == own:
            return
        s = source(step)
        got = gathered.at[block(s, at_fast, core)]
        send(got, got, ag_send.at[step], ag_recv.at[step], name(outward, at_fast, core)).wait_recv()

        @pl.when(inner)
        def _():
            if step == 0:
                to_slow_chip(s, across, 2, 2).start()
            else:
                to_slow_chip(s, outward, 2 + step, step).start()

        along_fast(s, step)
        to_partner(s, at_fast, step * fast)

    def take_fast(step):
        for off in range(1, fast):
            f = fast_at(fast - off)
            got = gathered.at[block(source(step), f, core)]
            send(got, got, fast_send.at[step, off], fast_recv.at[step, off], name(at_slow, f, core)).wait_recv()
            to_partner(source(step), f, step * fast + off)

    def take_core(step):
        for off in range(fast):
            slot = step * fast + off
            got = gathered.at[block(source(step), fast_at(fast - off), 1 - core)]
            send(got, got, core_send.at[slot], core_recv.at[slot], name(at_slow, at_fast, 1 - core)).wait_recv()

    def chunk(step):
        return pl.ds(pl.multiple_of(source(step) * chunk_rows, chunk_rows), chunk_rows)

    def half_expert(steps):
        expert = chip.astype(jnp.float32)
        factors = []
        for step in steps:
            info = gathered[chunk(step), edge:].astype(jnp.float32)
            factor = jnp.zeros((chunk_rows, 1), jnp.float32)
            for k in range(top):
                col = width - edge + k
                value = info[:, col + top : col + top + 1] + info[:, col + 2 * top : col + 2 * top + 1]
                factor += jnp.where(info[:, col : col + 1] == expert, value, 0.0)
            factors.append(factor)
        x = jnp.concatenate([gathered[chunk(step), :width] for step in steps], axis=0)
        pieces = []
        for low_col, high_col in column_cuts(hidden_count, 256):
            g = lax.dot_general(x, vm_gate[low_col:high_col, :], NT, preferred_element_type=jnp.float32)
            u = lax.dot_general(x, vm_up[low_col:high_col, :], NT, preferred_element_type=jnp.float32)
            pieces.append((jax.nn.silu(g) * u).astype(jnp.bfloat16))
        hidden = jnp.concatenate(pieces, axis=1)
        if steps[0] == own:
            weights[2].wait()
        for low_col, high_col in column_cuts(width, 512):
            y = jnp.dot(hidden, vm_down[:, low_col:high_col], preferred_element_type=jnp.float32)
            for i, step in enumerate(steps):
                part = y[i * chunk_rows : (i + 1) * chunk_rows] * factors[i]
                partial[chunk(step), low_col:high_col] = part.astype(jnp.bfloat16)

    def pair(s, c):
        return pl.ds(pl.multiple_of((s * 2 + c) * fast * rows, rows), fast * rows)

    def tile(index):
        return pl.ds(pl.multiple_of(index * rows, rows), rows)

    def core_copy(step):
        s = source(step)
        return send(
            partial.at[pair(s, 1 - core)], from_core.at[pl.ds(step * fast * rows, fast * rows)],
            pass_send.at[step], pass_recv.at[step], name(at_slow, at_fast, 1 - core),
        )

    def both_cores(step, f):
        s = source(step)
        mine_part = partial[block(s, f, core), :].astype(jnp.float32)
        return mine_part + from_core[tile(step * fast + f), :].astype(jnp.float32)

    def fast_copy(step, off):
        place = pl.ds((step * (fast - 1) + off - 1) * rows, rows)
        return send(
            to_fast.at[place], from_fast.at[place],
            give_send.at[step, off], give_recv.at[step, off], name(at_slow, fast_at(off), core),
        )

    def slow_copy(step):
        return send(
            to_slow.at[pl.ds(step * rows, rows)], from_slow.at[tile(at_slow)],
            slow_send.at[step], slow_recv.at[at_slow], name(source(step), at_fast, core),
        )

    def give_fast(step):
        core_copy(step).wait_recv()
        for off in range(1, fast):
            place = (step * (fast - 1) + off - 1) * rows
            to_fast[place : place + rows, :] = both_cores(step, fast_at(off)).astype(jnp.bfloat16)
            launch(fast_copy(step, off))

    first, second = order[: slow // 2], order[slow // 2 :]
    take_slow(0)
    take_slow(1)
    take_fast(own)
    take_fast(0)
    take_slow(2)
    take_fast(1)
    for step in first:
        take_core(step)
    weights[0].wait()
    weights[1].wait()
    half_expert(first)
    for step in first[1:] + first[:1]:
        launch(core_copy(step))
    take_fast(2)
    for step in first[1:] + first[:1]:
        give_fast(step)
    for step in second:
        take_core(step)
    half_expert(second)
    for step in second[::-1]:
        launch(core_copy(step))

    def finish(step):
        total = both_cores(step, at_fast)
        for off in range(1, fast):
            fast_copy(step, off).wait_recv()
            place = (step * (fast - 1) + off - 1) * rows
            total += from_fast[place : place + rows, :].astype(jnp.float32)
        if step == own:
            return total
        to_slow[step * rows : (step + 1) * rows, :] = total.astype(jnp.bfloat16)
        launch(slow_copy(step))

    finish(0)
    for step in second[::-1]:
        give_fast(step)
    for step in second[::-1]:
        finish(step)
    total = finish(own)
    for off in range(1, slow):
        s = slow_at(off)
        got = from_slow.at[tile(s)]
        send(got, got, slow_send.at[0], slow_recv.at[s], name(s, at_fast, core)).wait_recv()
        total += from_slow[tile(s), :].astype(jnp.float32)
    out[...] = total.astype(out.dtype)
    for copy in started:
        copy.wait_send()
    to_slow_chip(at_slow, outward, 0, 0).wait_send()

    @pl.when(inner)
    def _():
        for sem in range(1, 5):
            to_slow_chip(at_slow, outward, sem, 0).wait_send()


def dense_local(slow, fast, tokens, routes, gate_fixed, gate_weight, up_weight, down_weight):
    rows, width = tokens.shape
    top = routes.shape[1]
    gate_weight = jnp.swapaxes(gate_weight, 1, 2)
    up_weight = jnp.swapaxes(up_weight, 1, 2)
    padded = -(-(width + 3 * top) // 128) * 128
    every = slow * fast * 2 * rows
    dma = pltpu.SemaphoreType.DMA
    half = slow * fast * rows
    vmem = pl.BlockSpec(memory_space=pltpu.VMEM)
    anywhere = pl.BlockSpec(memory_space=pl.ANY)
    return pl.pallas_call(
        functools.partial(dense_kernel, slow, fast),
        out_shape=jax.ShapeDtypeStruct((rows, width), jnp.bfloat16),
        in_specs=[vmem, vmem, vmem, anywhere, anywhere, anywhere],
        out_specs=vmem,
        scratch_shapes=[
            pltpu.VMEM((every, padded), jnp.bfloat16),
            pltpu.VMEM(gate_weight.shape[1:], jnp.bfloat16),
            pltpu.VMEM(up_weight.shape[1:], jnp.bfloat16),
            pltpu.VMEM(down_weight.shape[1:], jnp.bfloat16),
            pltpu.VMEM((every, width), jnp.bfloat16),
            pltpu.VMEM((half, width), jnp.bfloat16),
            pltpu.VMEM((slow * (fast - 1) * rows, width), jnp.bfloat16),
            pltpu.VMEM((slow * (fast - 1) * rows, width), jnp.bfloat16),
            pltpu.VMEM(((slow - 1) * rows, width), jnp.bfloat16),
            pltpu.VMEM((slow * rows, width), jnp.bfloat16),
            dma((3,)),
            dma((5,)), dma((3,)),
            dma((slow * fast,)), dma((slow * fast,)),
            dma((slow, fast)), dma((slow, fast)),
            dma((slow,)), dma((slow,)),
            dma((slow,)), dma((slow,)),
            dma((slow, fast)), dma((slow, fast)),
        ],
        compiler_params=pltpu.CompilerParams(
            collective_id=0, has_side_effects=True, vmem_limit_bytes=60 * 2**20
        ),
    )(tokens, routes.T, gate_fixed.T, gate_weight, up_weight, down_weight)


def solution(mesh):
    placed = (
        P(("groups", "ep"), None),
        P(("groups", "ep"), None),
        P(("groups", "ep"), None),
        P("ep", None, None),
        P("ep", None, None),
        P("ep", None, None),
    )
    chips = mesh.shape["ep"] // 2

    def body(*args):
        top = args[1].shape[1]
        if chips <= 4 * top and chips % 4 == 0:
            return dense_local(4, chips // 4, *args)
        return local(*args)

    return jax.shard_map(
        body, mesh=mesh, in_specs=placed, out_specs=P(("groups", "ep"), None), check_vma=False
    )
```

profile of v0, /device:TPU:0, one launch (start us, length us, event | category | flops | bytes accessed | tf_op | source)
XLA Modules:
  0.0 40.2 jit_solution(14119719956833897195)
XLA Ops:
  0.0 38.7 %shard_map.64 = bf16[16,2880]{1,0:T(8,128)(2,1)} custom-call(bf16[16,2880]{1,0:T(8,128)(2,1)} %tokens.1, s32[4,16]{1,0:T(4,128)} %bitcast.6, s32[4,16]{1,0:T(4,128)} %bitcast.7, bf16[1,720,2880]{2,1,0:T(8,128)(2,1)} %bitcast.4, bf16[1,720,2880]{2,1,0:T(8,128)(2,1)} %bitcast.5, bf16[1,720,2880]{2,1,0:T(8,128)(2,1)} %w_down.1), custom_call_target="tpu_custom_call" | custom-call | tf_op jit(solution)/shard_map/pallas_call | solution.py:344
  38.7 1.5 %copy.8 = bf16[16,2880]{1,0:T(8,128)(2,1)} copy(bf16[16,2880]{1,0:T(8,128)(2,1)} %shard_map.64) | data formatting | bytes 184320
where the time goes:
time: 40.4 us; the launch traced here: 40.2 us
  Pallas kernels  38.7 us (96%)
  local copies, waits for them, and re-layouts  1.54 us (4%)
    pallas_call x1, Pallas kernels, dense_local(): pl.pallas_call(functools.partial(dense_kernel, slow, fast), out_shape=jax...  38.7 us
    unnamed x1, local copies, waits for them, and re-layouts  1.54 us

commit v1 on v0

v1 whole, which is shorter than its diff:
```python
import jax
import jax.numpy as jnp
from jax import lax
from jax.experimental import pallas as pl
from jax.experimental.pallas import tpu as pltpu
from jax.sharding import PartitionSpec as P


def swapped(value, axis, bit):
    mask = 2**bit
    pairs = [(source, source ^ mask) for source in range(lax.axis_size(axis))]
    return lax.ppermute(value, axis, pairs)


def expert_half(expert_rows, w_gate, w_up, w_down):
    gate_part = jnp.dot(expert_rows, w_gate, preferred_element_type=jnp.float32)
    up_part = jnp.dot(expert_rows, w_up, preferred_element_type=jnp.float32)
    hidden = (jax.nn.silu(gate_part) * up_part).astype(jnp.bfloat16)
    return jnp.dot(hidden, w_down, preferred_element_type=jnp.float32).astype(jnp.bfloat16)


def local(tokens, routes, gate_fixed, gate_weight, up_weight, down_weight):
    devices_ep = lax.axis_size("ep")
    experts = devices_ep // 2
    tok_count = tokens.shape[0]
    top_count = routes.shape[1]
    width = tokens.shape[1]
    capacity = 2 * tok_count * top_count // experts
    onehot = (routes[:, :, None] == jnp.arange(experts, dtype=jnp.int32)).astype(jnp.int32)
    flat_hot = onehot.reshape(tok_count * top_count, experts)
    before = jnp.cumsum(flat_hot, axis=0) - flat_hot
    position = jnp.sum(before * flat_hot, axis=1).reshape(tok_count, top_count)
    slot_index = routes * capacity + position
    select = (slot_index[:, :, None] == jnp.arange(experts * capacity, dtype=jnp.int32)).astype(
        jnp.int32
    )
    select = jnp.sum(select, axis=1).astype(jnp.bfloat16)
    packed = jnp.einsum("ts,td->sd", select, tokens, preferred_element_type=jnp.float32).astype(
        jnp.bfloat16
    )
    packed = packed.reshape(experts, 1, capacity, width)
    outgoing = jnp.broadcast_to(packed, (experts, 2, capacity, width)).reshape(
        devices_ep, capacity, width
    )
    received = lax.all_to_all(outgoing, "ep", split_axis=0, concat_axis=0, tiled=True)
    result = expert_half(received.reshape(-1, width), gate_weight[0], up_weight[0], down_weight[0])
    partial_value = result.reshape(received.shape[0], received.shape[1], width)
    parity = lax.axis_index("ep") % 2
    halves = partial_value.reshape(devices_ep, capacity, 2, width // 2)
    kept_half = lax.dynamic_index_in_dim(halves, parity, 2, keepdims=False)
    given_half = lax.dynamic_index_in_dim(halves, 1 - parity, 2, keepdims=False)
    partner = swapped(given_half, "ep", 0)
    reduced = (kept_half.astype(jnp.float32) + partner.astype(jnp.float32)).astype(jnp.bfloat16)
    returned = lax.all_to_all(reduced, "ep", split_axis=0, concat_axis=0, tiled=True)
    ordered = returned.reshape(experts, 2, capacity, width // 2).transpose(0, 2, 1, 3)
    expert_out = ordered.reshape(experts * capacity, width)
    picked = jnp.take(expert_out, slot_index.reshape(-1), axis=0).reshape(
        tok_count, top_count, width
    )
    weights = gate_fixed.astype(jnp.float32) / 65536.0
    mixed = jnp.sum(weights[:, :, None] * picked.astype(jnp.float32), axis=1)
    return mixed.astype(jnp.bfloat16)


NT = (((1,), (1,)), ((), ()))
TN = (((0,), (0,)), ((), ()))


def column_cuts(width, step):
    return [(low, min(low + step, width)) for low in range(0, width, step)]


def quad_kernel(
    tokens, routes, gates, w_gate, w_up, w_down, out,
    own_tokens, own_routes, own_gates, gathered, vm_gate, vm_up, vm_down, gate_sum, up_sum, partial, from_core,
    to_quad, from_quad, kept, to_far, from_far,
    in_sem, w_sem, ag_send, ag_recv, core_send, core_recv, quad_send, quad_recv, far_send, far_recv,
):
    rows, width = own_tokens.shape
    top = own_routes.shape[0]
    padded = gathered.shape[1]
    hidden_count = vm_gate.shape[0]
    device = lax.axis_index("ep")
    expert = (device // 2).astype(jnp.float32)

    def other(mask):
        return device + mask * (1 - 2 * lax.rem(device // mask, 2))

    core_peer = other(1)
    far_peer = other(8)
    side_peer = other(2)
    pair_peer = other(4)
    diagonal = side_peer + pair_peer - device
    quad_peers = [None, side_peer, pair_peer, diagonal]

    def send(source, target, send_sem, recv_sem, device_id):
        return pltpu.make_async_remote_copy(
            src_ref=source, dst_ref=target, send_sem=send_sem, recv_sem=recv_sem,
            device_id={"ep": device_id}, device_id_type=pl.DeviceIdType.MESH,
        )

    peers = [core_peer, side_peer, pair_peer, diagonal, far_peer]
    barrier = pltpu.get_barrier_semaphore()
    for peer in peers:
        pl.semaphore_signal(
            barrier, inc=1, device_id={"ep": peer}, device_id_type=pl.DeviceIdType.MESH
        )

    inputs = [
        pltpu.make_async_copy(source, target, in_sem.at[i])
        for i, (source, target) in enumerate(
            ((tokens, own_tokens), (routes, own_routes), (gates, own_gates))
        )
    ]
    weights = [
        pltpu.make_async_copy(source.at[0], target, w_sem.at[i])
        for i, (source, target) in enumerate(((w_gate, vm_gate), (w_up, vm_up), (w_down, vm_down)))
    ]
    for copy in inputs:
        copy.start()

    block_rows = 4 * rows
    chunk_rows = 2 * block_rows
    edge = width // 128 * 128
    step = -(-(padded // 128) // PIECES) * 128
    cuts = column_cuts(padded, step)

    def slot(chunk, core, q):
        return pl.ds(chunk * chunk_rows + core * block_rows + q * rows, rows)

    for copy in inputs:
        copy.wait()
    for copy in weights:
        copy.start()
    lanes = lax.broadcasted_iota(jnp.int32, (rows, padded - edge), 1) + edge
    mine = slot(0, 0, 0)
    partial[:, edge:] = jnp.zeros((2 * chunk_rows, padded - edge), jnp.bfloat16)
    gathered[mine, :edge] = own_tokens[:, :edge]
    gathered[mine, edge:] = jnp.zeros((rows, padded - edge), jnp.bfloat16)
    gathered[mine, edge:width] = own_tokens[:, edge:]
    scale = jnp.transpose(own_gates[...].astype(jnp.float32)) / 65536.0
    high = scale.astype(jnp.bfloat16).astype(jnp.float32)
    low = scale - high
    ids = jnp.transpose(own_routes[...].astype(jnp.float32))
    tail = gathered[mine, edge:].astype(jnp.float32)
    for k in range(top):
        tail = jnp.where(lanes == width + k, ids[:, k : k + 1], tail)
        tail = jnp.where(lanes == width + top + k, high[:, k : k + 1], tail)
        tail = jnp.where(lanes == width + 2 * top + k, low[:, k : k + 1], tail)
    gathered[mine, edge:] = tail.astype(jnp.bfloat16)

    with jax.named_scope("barrier"):
        pl.semaphore_wait(barrier, len(peers))

    started = []

    def launch(copy):
        copy.start()
        started.append(copy)

    def moved(chunk, core, q, piece, origin, peer):
        low_col, high_col = cuts[piece]
        return send(
            gathered.at[origin, low_col:high_col], gathered.at[slot(chunk, core, q), low_col:high_col],
            ag_send.at[chunk, core, q, piece], ag_recv.at[chunk, core, q, piece], peer,
        )

    def arrived(chunk, core, q, piece):
        moved(chunk, core, q, piece, slot(chunk, core, q), core_peer).wait_recv()

    def to_core(chunk, q, piece):
        launch(moved(chunk, 1, q, piece, slot(chunk, 0, q), core_peer))

    pieces = range(len(cuts))
    for piece in pieces:
        launch(moved(1, 0, 0, piece, mine, far_peer))
    for piece in pieces:
        for q in (2, 1) if RELAY else (2, 1, 3):
            launch(moved(0, 0, q, piece, mine, quad_peers[q]))
        to_core(0, 0, piece)

    def take_near(piece):
        for q in (2, 1) if RELAY else (2, 1, 3):
            arrived(0, 0, q, piece)
            if RELAY and q == 2:
                launch(moved(0, 0, 3, piece, slot(0, 0, 2), side_peer))
            to_core(0, q, piece)

    def take_far(piece):
        arrived(1, 0, 0, piece)
        for q in (3, 2, 1):
            launch(moved(1, 0, q, piece, slot(1, 0, 0), quad_peers[q]))
        to_core(1, 0, piece)

    def chunk_slice(chunk):
        return pl.ds(chunk * chunk_rows, chunk_rows)

    def core_copy(chunk, piece):
        low_col, high_col = cuts[piece]
        start = chunk * chunk_rows
        return send(
            partial.at[pl.ds(start + block_rows, block_rows), low_col:high_col],
            from_core.at[pl.ds(chunk * block_rows, block_rows), low_col:high_col],
            core_send.at[chunk, piece], core_recv.at[chunk, piece], core_peer,
        )

    def add_products(piece):
        low_col, high_col = cuts[piece][0], min(cuts[piece][1], width)
        x = gathered[:, low_col:high_col]
        for weight, total in ((vm_gate, gate_sum), (vm_up, up_sum)):
            product = lax.dot_general(
                weight[:, low_col:high_col], x, NT, preferred_element_type=jnp.float32
            )
            total[...] = product if piece == 0 else total[...] + product

    def gate_factor():
        info = gathered[:, edge:].astype(jnp.float32)
        factor = jnp.zeros((2 * chunk_rows, 1), jnp.float32)
        for k in range(top):
            col = width - edge + k
            value = info[:, col + top : col + top + 1] + info[:, col + 2 * top : col + 2 * top + 1]
            factor += jnp.where(info[:, col : col + 1] == expert, value, 0.0)
        return factor

    def run_down(hidden, factor, piece):
        start, stop = cuts[piece]
        for low_col in range(start, min(stop, width), 512):
            high_col = min(low_col + 512, stop, width)
            y = lax.dot_general(
                hidden, vm_down[:, low_col:high_col], TN, preferred_element_type=jnp.float32
            )
            partial[:, low_col:high_col] = (y * factor).astype(jnp.bfloat16)
        for chunk in (1, 0):
            launch(core_copy(chunk, piece))

    def quad_slot(chunk, q):
        return pl.ds((chunk * 3 + q - 1) * rows, rows)

    def quad_copy(chunk, q, piece):
        low_col, high_col = cuts[piece]
        where = quad_slot(chunk, q)
        return send(
            to_quad.at[where, low_col:high_col], from_quad.at[where, low_col:high_col],
            quad_send.at[chunk, q, piece], quad_recv.at[chunk, q, piece], quad_peers[q],
        )

    def give_quad(chunk, piece):
        low_col, high_col = cuts[piece]
        core_copy(chunk, piece).wait_recv()
        for q in (3, 2, 1, 0):
            total = partial[slot(chunk, 0, q), low_col:high_col].astype(jnp.float32)
            total += from_core[pl.ds(chunk * block_rows + q * rows, rows), low_col:high_col].astype(jnp.float32)
            if q == 0:
                kept[pl.ds(chunk * rows, rows), low_col:high_col] = total
            else:
                to_quad[quad_slot(chunk, q), low_col:high_col] = total.astype(jnp.bfloat16)
                launch(quad_copy(chunk, q, piece))

    def quad_total(chunk, piece):
        low_col, high_col = cuts[piece]
        total = kept[pl.ds(chunk * rows, rows), low_col:high_col]
        for q in (1, 2, 3):
            quad_copy(chunk, q, piece).wait_recv()
            total += from_quad[quad_slot(chunk, q), low_col:high_col].astype(jnp.float32)
        return total

    def far_copy(piece):
        low_col, high_col = cuts[piece]
        return send(
            to_far.at[:, low_col:high_col], from_far.at[:, low_col:high_col],
            far_send.at[piece], far_recv.at[piece], far_peer,
        )

    def take_quad(piece):
        if RELAY:
            arrived(0, 0, 3, piece)
            to_core(0, 3, piece)
        for q in (1, 2, 3):
            arrived(1, 0, q, piece)
            to_core(1, q, piece)

    def take_core(piece):
        for chunk in (0, 1):
            for q in range(4):
                arrived(chunk, 1, q, piece)

    last = len(cuts) - 1
    for piece in pieces:
        with jax.named_scope(f"near{piece}"):
            take_near(piece)
        with jax.named_scope(f"far{piece}"):
            take_far(piece)
        if piece > 0:
            with jax.named_scope(f"quad{piece - 1}"):
                take_quad(piece - 1)
    weights[0].wait()
    weights[1].wait()
    for piece in pieces:
        with jax.named_scope(f"core{piece}"):
            take_core(piece)
        with jax.named_scope(f"dot{piece}"):
            add_products(piece)
        if piece == last - 1:
            with jax.named_scope(f"quad{last}"):
                take_quad(last)
    with jax.named_scope("silu"):
        hidden = (jax.nn.silu(gate_sum[...]) * up_sum[...]).astype(jnp.bfloat16)
        factor = gate_factor()
    weights[2].wait()
    for piece in pieces:
        with jax.named_scope(f"down{piece}"):
            run_down(hidden, factor, piece)
    with jax.named_scope("give1"):
        for piece in pieces:
            give_quad(1, piece)
    with jax.named_scope("give0"):
        for piece in pieces:
            give_quad(0, piece)
    with jax.named_scope("far_out"):
        for piece in pieces:
            low_col, high_col = cuts[piece]
            to_far[:, low_col:high_col] = quad_total(1, piece).astype(jnp.bfloat16)
            launch(far_copy(piece))
    with jax.named_scope("final"):
        for piece in pieces:
            low_col, high_col = cuts[piece]
            total = quad_total(0, piece)
            far_copy(piece).wait_recv()
            total += from_far[:, low_col:high_col].astype(jnp.float32)
            high_col = min(high_col, width)
            out[:, low_col:high_col] = total[:, : high_col - low_col].astype(out.dtype)
    for copy in started:
        copy.wait_send()


PIECES = 3
RELAY = True


def quad_local(tokens, routes, gate_fixed, gate_weight, up_weight, down_weight):
    rows, width = tokens.shape
    top = routes.shape[1]
    gate_weight = jnp.swapaxes(gate_weight, 1, 2)
    up_weight = jnp.swapaxes(up_weight, 1, 2)
    padded = -(-(width + 3 * top) // 128) * 128
    dma = pltpu.SemaphoreType.DMA
    anywhere = pl.BlockSpec(memory_space=pl.ANY)
    routes, gate_fixed = routes.T, gate_fixed.T
    return pl.pallas_call(
        quad_kernel,
        out_shape=pltpu.VMEM((rows, width), jnp.bfloat16),
        in_specs=[anywhere] * 6,
        out_specs=pl.BlockSpec(memory_space=pltpu.VMEM),
        scratch_shapes=[
            pltpu.VMEM(tokens.shape, jnp.bfloat16),
            pltpu.VMEM(routes.shape, jnp.int32),
            pltpu.VMEM(gate_fixed.shape, jnp.int32),
            pltpu.VMEM((16 * rows, padded), jnp.bfloat16),
            pltpu.VMEM(gate_weight.shape[1:], jnp.bfloat16),
            pltpu.VMEM(up_weight.shape[1:], jnp.bfloat16),
            pltpu.VMEM(down_weight.shape[1:], jnp.bfloat16),
            pltpu.VMEM((gate_weight.shape[1], 16 * rows), jnp.float32),
            pltpu.VMEM((gate_weight.shape[1], 16 * rows), jnp.float32),
            pltpu.VMEM((16 * rows, padded), jnp.bfloat16),
            pltpu.VMEM((8 * rows, padded), jnp.bfloat16),
            pltpu.VMEM((6 * rows, padded), jnp.bfloat16),
            pltpu.VMEM((6 * rows, padded), jnp.bfloat16),
            pltpu.VMEM((2 * rows, padded), jnp.float32),
            pltpu.VMEM((rows, padded), jnp.bfloat16),
            pltpu.VMEM((rows, padded), jnp.bfloat16),
            dma((3,)), dma((3,)),
            dma((2, 2, 4, PIECES)), dma((2, 2, 4, PIECES)),
            dma((2, PIECES)), dma((2, PIECES)),
            dma((2, 4, PIECES)), dma((2, 4, PIECES)),
            dma((PIECES,)), dma((PIECES,)),
        ],
        compiler_params=pltpu.CompilerParams(
            collective_id=0, has_side_effects=True, vmem_limit_bytes=60 * 2**20
        ),
    )(tokens, routes, gate_fixed, gate_weight, up_weight, down_weight)


def solution(mesh):
    placed = (
        P(("groups", "ep"), None),
        P(("groups", "ep"), None),
        P(("groups", "ep"), None),
        P("ep", None, None),
        P("ep", None, None),
        P("ep", None, None),
    )
    chips = mesh.shape["ep"] // 2

    def body(*args):
        if chips == 2**3:
            return quad_local(*args)
        return local(*args)

    return jax.shard_map(
        body, mesh=mesh, in_specs=placed, out_specs=P(("groups", "ep"), None), check_vma=False
    )
```

time: 40.4 us -> 35.4 us (0.88)
  Pallas kernels: 38.7 us -> 34.6 us
  local copies, waits for them, and re-layouts: 1.54 us -> 0.64 us
    pallas_call x1, Pallas kernels: 38.7 us -> 34.6 us  [quad_local(): pl.pallas_call(quad_kernel, out_shape=pltpu.VMEM((rows, width), jnp.bfloa...]
    unnamed x1, local copies, waits for them, and re-layouts: 1.54 us -> 0.64 us
where the time goes in v1:
time: 35.4 us; the launch traced here: 35.3 us
  Pallas kernels  34.6 us (98%)
  local copies, waits for them, and re-layouts  0.64 us (2%)
    pallas_call x1, Pallas kernels, quad_local(): pl.pallas_call(quad_kernel, out_shape=pltpu.VMEM((rows, width), jnp.bfloa...  34.6 us

profile of v1, /device:TPU:0, one launch (start us, length us, event | category | flops | bytes accessed | tf_op | source)
XLA Modules:
  0.0 35.3 jit_solution(13650298764353481505)
XLA Ops:
  0.0 34.6 %shard_map.64 = bf16[16,2880]{1,0:T(8,128)(2,1)S(1)} custom-call(bf16[16,2880]{1,0:T(8,128)(2,1)} %tokens.1, s32[4,16]{1,0:T(4,128)} %bitcast.6, s32[4,16]{1,0:T(4,128)} %bitcast.7, bf16[1,720,2880]{2,1,0:T(8,128)(2,1)} %bitcast.4, bf16[1,720,2880]{2,1,0:T(8,128)(2,1)} %bitcast.5, bf16[1,720,2880]{2,1,0:T(8,128)(2,1)} %w_down.1), custom_call_target="tpu_custom_call" | custom-call | tf_op jit(solution)/shard_map/pallas_call | solution.py:349
  34.6 0.6 %copy.8 = bf16[16,2880]{1,0:T(8,128)(2,1)} copy(bf16[16,2880]{1,0:T(8,128)(2,1)S(1)} %shard_map.64) | data formatting | bytes 184320

commit v2 on v1

v2 whole, which is shorter than its diff:
```python
import jax
import jax.numpy as jnp
from jax import lax
from jax.experimental import pallas as pl
from jax.experimental.pallas import tpu as pltpu
from jax.sharding import PartitionSpec as P


def swapped(value, axis, bit):
    mask = 2**bit
    pairs = [(source, source ^ mask) for source in range(lax.axis_size(axis))]
    return lax.ppermute(value, axis, pairs)


def expert_half(expert_rows, w_gate, w_up, w_down):
    gate_part = jnp.dot(expert_rows, w_gate, preferred_element_type=jnp.float32)
    up_part = jnp.dot(expert_rows, w_up, preferred_element_type=jnp.float32)
    hidden = (jax.nn.silu(gate_part) * up_part).astype(jnp.bfloat16)
    return jnp.dot(hidden, w_down, preferred_element_type=jnp.float32).astype(jnp.bfloat16)


def local(tokens, routes, gate_fixed, gate_weight, up_weight, down_weight):
    devices_ep = lax.axis_size("ep")
    experts = devices_ep // 2
    tok_count = tokens.shape[0]
    top_count = routes.shape[1]
    width = tokens.shape[1]
    capacity = 2 * tok_count * top_count // experts
    onehot = (routes[:, :, None] == jnp.arange(experts, dtype=jnp.int32)).astype(jnp.int32)
    flat_hot = onehot.reshape(tok_count * top_count, experts)
    before = jnp.cumsum(flat_hot, axis=0) - flat_hot
    position = jnp.sum(before * flat_hot, axis=1).reshape(tok_count, top_count)
    slot_index = routes * capacity + position
    select = (slot_index[:, :, None] == jnp.arange(experts * capacity, dtype=jnp.int32)).astype(
        jnp.int32
    )
    select = jnp.sum(select, axis=1).astype(jnp.bfloat16)
    packed = jnp.einsum("ts,td->sd", select, tokens, preferred_element_type=jnp.float32).astype(
        jnp.bfloat16
    )
    packed = packed.reshape(experts, 1, capacity, width)
    outgoing = jnp.broadcast_to(packed, (experts, 2, capacity, width)).reshape(
        devices_ep, capacity, width
    )
    received = lax.all_to_all(outgoing, "ep", split_axis=0, concat_axis=0, tiled=True)
    result = expert_half(received.reshape(-1, width), gate_weight[0], up_weight[0], down_weight[0])
    partial_value = result.reshape(received.shape[0], received.shape[1], width)
    parity = lax.axis_index("ep") % 2
    halves = partial_value.reshape(devices_ep, capacity, 2, width // 2)
    kept_half = lax.dynamic_index_in_dim(halves, parity, 2, keepdims=False)
    given_half = lax.dynamic_index_in_dim(halves, 1 - parity, 2, keepdims=False)
    partner = swapped(given_half, "ep", 0)
    reduced = (kept_half.astype(jnp.float32) + partner.astype(jnp.float32)).astype(jnp.bfloat16)
    returned = lax.all_to_all(reduced, "ep", split_axis=0, concat_axis=0, tiled=True)
    ordered = returned.reshape(experts, 2, capacity, width // 2).transpose(0, 2, 1, 3)
    expert_out = ordered.reshape(experts * capacity, width)
    picked = jnp.take(expert_out, slot_index.reshape(-1), axis=0).reshape(
        tok_count, top_count, width
    )
    weights = gate_fixed.astype(jnp.float32) / 65536.0
    mixed = jnp.sum(weights[:, :, None] * picked.astype(jnp.float32), axis=1)
    return mixed.astype(jnp.bfloat16)


NT = (((1,), (1,)), ((), ()))
TN = (((0,), (0,)), ((), ()))


def column_cuts(low, high, step):
    return [(start, min(start + step, high)) for start in range(low, high, step)]


def portions(padded, shares):
    tiles = padded // 128
    ends = [tiles * sum(shares[:i]) // sum(shares) * 128 for i in range(len(shares) + 1)]
    return list(zip(ends[:-1], ends[1:]))


NT = (((1,), (1,)), ((), ()))
TN = (((0,), (0,)), ((), ()))
IN_SHARES = (8, 8, 7)
OUT_SHARES = (8, 8, 7)


def quad_kernel(
    tokens, routes, gates, w_gate, w_up, w_down, out,
    own_tokens, own_routes, own_gates, gathered, vm_gate, vm_up, vm_down, gate_sum, up_sum, partial,
    from_core, to_quad, from_quad, kept, to_far, from_far,
    in_sem, w_sem, sent, near_sem, far_sem, late_sem, core_sem,
    pass_sem, quad_sem, side_sem, own_sem, back_sem,
):
    rows, width = own_tokens.shape
    top = own_routes.shape[0]
    padded = gathered.shape[1]
    device = lax.axis_index("ep")
    expert = (device // 2).astype(jnp.float32)

    def other(mask):
        return device + mask * (1 - 2 * lax.rem(device // mask, 2))

    core_peer = other(1)
    side_peer = other(2)
    pair_peer = other(4)
    far_peer = other(8)
    diagonal = side_peer + pair_peer - device
    quad_peers = [None, side_peer, pair_peer, diagonal]

    peers = [core_peer, side_peer, pair_peer, diagonal, far_peer]
    barrier = pltpu.get_barrier_semaphore()
    for peer in peers:
        pl.semaphore_signal(
            barrier, inc=1, device_id={"ep": peer}, device_id_type=pl.DeviceIdType.MESH
        )

    inputs = [
        pltpu.make_async_copy(source, target, in_sem.at[i])
        for i, (source, target) in enumerate(
            ((tokens, own_tokens), (routes, own_routes), (gates, own_gates))
        )
    ]
    weights = [
        pltpu.make_async_copy(source.at[0], target, w_sem.at[i])
        for i, (source, target) in enumerate(((w_gate, vm_gate), (w_up, vm_up), (w_down, vm_down)))
    ]
    for copy in inputs:
        copy.start()

    block_rows = 4 * rows
    chunk_rows = 2 * block_rows
    edge = width // 128 * 128
    cuts = portions(padded, IN_SHARES)
    out_cuts = portions(padded, OUT_SHARES)
    pieces = range(len(cuts))
    out_pieces = range(len(out_cuts))

    def slot(chunk, core, q):
        return pl.ds(chunk * chunk_rows + core * block_rows + q * rows, rows)

    for copy in inputs:
        copy.wait()
    for copy in weights:
        copy.start()
    lanes = lax.broadcasted_iota(jnp.int32, (rows, padded - edge), 1) + edge
    mine = slot(0, 0, 0)
    partial[:, edge:] = jnp.zeros((2 * chunk_rows, padded - edge), jnp.bfloat16)
    gathered[mine, :edge] = own_tokens[:, :edge]
    gathered[mine, edge:] = jnp.zeros((rows, padded - edge), jnp.bfloat16)
    gathered[mine, edge:width] = own_tokens[:, edge:]
    scale = jnp.transpose(own_gates[...].astype(jnp.float32)) / 65536.0
    high = scale.astype(jnp.bfloat16).astype(jnp.float32)
    low = scale - high
    ids = jnp.transpose(own_routes[...].astype(jnp.float32))
    tail = gathered[mine, edge:].astype(jnp.float32)
    for k in range(top):
        tail = jnp.where(lanes == width + k, ids[:, k : k + 1], tail)
        tail = jnp.where(lanes == width + top + k, high[:, k : k + 1], tail)
        tail = jnp.where(lanes == width + 2 * top + k, low[:, k : k + 1], tail)
    gathered[mine, edge:] = tail.astype(jnp.bfloat16)

    with jax.named_scope("barrier"):
        pl.semaphore_wait(barrier, len(peers))

    def remote(source, target, send_sem, recv_sem, device_id):
        return pltpu.make_async_remote_copy(
            src_ref=source, dst_ref=target, send_sem=send_sem, recv_sem=recv_sem,
            device_id={"ep": device_id}, device_id_type=pl.DeviceIdType.MESH,
        )

    sizes = [0, 0]

    def launch(kind, source, target, recv_sem, peer):
        remote(source, target, sent.at[kind], recv_sem, peer).start()
        sizes[kind] += source.shape[0] * source.shape[1]

    def await_rows(buffer, count, cut, recv_sem):
        where = buffer.at[pl.ds(0, count * rows), cut[0] : cut[1]]
        remote(where, where, recv_sem, recv_sem, core_peer).wait_recv()

    def await_sent(kind):
        rows_sent = sizes[kind] // padded
        assert rows_sent * padded == sizes[kind]
        where = gathered.at[pl.ds(0, rows_sent), :]
        remote(where, where, sent.at[kind], sent.at[kind], core_peer).wait_send()

    def give(origin, chunk, core, q, piece, recv_sem, peer):
        cut = cuts[piece]
        launch(
            0, gathered.at[origin, cut[0] : cut[1]],
            gathered.at[slot(chunk, core, q), cut[0] : cut[1]], recv_sem.at[piece], peer,
        )

    def to_core(chunk, q, piece):
        give(slot(chunk, 0, q), chunk, 1, q, piece, core_sem, core_peer)

    for piece in pieces:
        give(mine, 1, 0, 0, piece, far_sem, far_peer)
        for q in (2, 1):
            give(mine, 0, 0, q, piece, near_sem, quad_peers[q])
        to_core(0, 0, piece)

    def take_near(piece):
        await_rows(gathered, 2, cuts[piece], near_sem.at[piece])
        give(slot(0, 0, 2), 0, 0, 3, piece, late_sem, side_peer)
        for q in (2, 1):
            to_core(0, q, piece)

    def take_far(piece):
        await_rows(gathered, 1, cuts[piece], far_sem.at[piece])
        for q in (3, 2, 1):
            give(slot(1, 0, 0), 1, 0, q, piece, late_sem, quad_peers[q])
        to_core(1, 0, piece)

    def take_late(piece):
        await_rows(gathered, 4, cuts[piece], late_sem.at[piece])
        to_core(0, 3, piece)
        for q in (1, 2, 3):
            to_core(1, q, piece)

    def add_products(piece):
        low_col, high_col = cuts[piece][0], min(cuts[piece][1], width)
        x = gathered[:, low_col:high_col]
        for weight, total in ((vm_gate, gate_sum), (vm_up, up_sum)):
            product = lax.dot_general(
                weight[:, low_col:high_col], x, NT, preferred_element_type=jnp.float32
            )
            total[...] = product if piece == 0 else total[...] + product

    def gate_factor():
        info = gathered[:, edge:].astype(jnp.float32)
        factor = jnp.zeros((2 * chunk_rows, 1), jnp.float32)
        for k in range(top):
            col = width - edge + k
            value = info[:, col + top : col + top + 1] + info[:, col + 2 * top : col + 2 * top + 1]
            factor += jnp.where(info[:, col : col + 1] == expert, value, 0.0)
        return factor

    def run_down(hidden, factor, piece):
        low_out, high_out = out_cuts[piece]
        for low_col, high_col in column_cuts(low_out, min(high_out, width), 512):
            y = lax.dot_general(
                hidden, vm_down[:, low_col:high_col], TN, preferred_element_type=jnp.float32
            )
            partial[:, low_col:high_col] = (y * factor).astype(jnp.bfloat16)
        for chunk in (1, 0):
            launch(
                1, partial.at[pl.ds(chunk * chunk_rows + block_rows, block_rows), low_out:high_out],
                from_core.at[pl.ds(chunk * block_rows, block_rows), low_out:high_out],
                pass_sem.at[piece], core_peer,
            )

    def chip_sum(chunk, q, piece):
        low_col, high_col = out_cuts[piece]
        mine_part = partial[slot(chunk, 0, q), low_col:high_col].astype(jnp.float32)
        where = pl.ds(chunk * block_rows + q * rows, rows)
        return mine_part + from_core[where, low_col:high_col].astype(jnp.float32)

    def give_sum(total, chunk, q, piece, recv_sem, peer):
        low_col, high_col = out_cuts[piece]
        where = pl.ds((chunk * 3 + q - 1) * rows, rows)
        to_quad[where, low_col:high_col] = total.astype(jnp.bfloat16)
        launch(
            1, to_quad.at[where, low_col:high_col], from_quad.at[where, low_col:high_col],
            recv_sem.at[piece], peer,
        )

    def got(chunk, q, piece):
        low_col, high_col = out_cuts[piece]
        return from_quad[pl.ds((chunk * 3 + q - 1) * rows, rows), low_col:high_col].astype(jnp.float32)

    def give_b(piece):
        low_col, high_col = out_cuts[piece]
        await_rows(gathered, 8, out_cuts[piece], pass_sem.at[piece])
        for q in (3, 1, 2):
            give_sum(chip_sum(1, q, piece), 1, q, piece, quad_sem, quad_peers[q])
        kept[pl.ds(rows, rows), low_col:high_col] = chip_sum(1, 0, piece)

    for piece in pieces:
        with jax.named_scope(f"near{piece}"):
            take_near(piece)
        with jax.named_scope(f"far{piece}"):
            take_far(piece)
    last = len(cuts) - 1
    with jax.named_scope("late0"):
        take_late(0)
    weights[0].wait()
    weights[1].wait()
    for piece in pieces:
        if piece < last:
            with jax.named_scope(f"late{piece + 1}"):
                take_late(piece + 1)
        with jax.named_scope(f"core{piece}"):
            await_rows(gathered, 8, cuts[piece], core_sem.at[piece])
        with jax.named_scope(f"dot{piece}"):
            if piece == last:
                factor = gate_factor()
            add_products(piece)
    with jax.named_scope("silu"):
        hidden = (jax.nn.silu(gate_sum[...]) * up_sum[...]).astype(jnp.bfloat16)
    weights[2].wait()
    for piece in out_pieces:
        with jax.named_scope(f"down{piece}"):
            run_down(hidden, factor, piece)
        if piece == GIVE_AT:
            with jax.named_scope("give1_0"):
                give_b(0)
    with jax.named_scope("give1"):
        for piece in out_pieces:
            if piece > 0 or GIVE_AT is None:
                give_b(piece)
    with jax.named_scope("give0"):
        for q, recv_sem in ((3, side_sem), (1, own_sem)):
            for piece in out_pieces:
                give_sum(chip_sum(0, q, piece), 0, q, piece, recv_sem, side_peer)
    with jax.named_scope("kept"):
        for piece in out_pieces:
            low_col, high_col = out_cuts[piece]
            kept[pl.ds(0, rows), low_col:high_col] = chip_sum(0, 0, piece)
            kept[pl.ds(2 * rows, rows), low_col:high_col] = chip_sum(0, 2, piece)
    for piece in out_pieces:
        low_col, high_col = out_cuts[piece]
        with jax.named_scope(f"far_out{piece}"):
            await_rows(gathered, 3, out_cuts[piece], quad_sem.at[piece])
            total = kept[pl.ds(rows, rows), low_col:high_col]
            total += got(1, 1, piece) + got(1, 2, piece) + got(1, 3, piece)
            to_far[:, low_col:high_col] = total.astype(jnp.bfloat16)
            launch(
                1, to_far.at[:, low_col:high_col], from_far.at[:, low_col:high_col],
                back_sem.at[piece], far_peer,
            )
    for piece in out_pieces:
        low_col, high_col = out_cuts[piece]
        with jax.named_scope(f"relay{piece}"):
            await_rows(gathered, 1, out_cuts[piece], side_sem.at[piece])
            total = kept[pl.ds(2 * rows, rows), low_col:high_col] + got(0, 3, piece)
            give_sum(total, 0, 2, piece, own_sem, pair_peer)
    with jax.named_scope("drain"):
        await_sent(0)
    for piece in out_pieces:
        low_col, high_col = out_cuts[piece]
        with jax.named_scope(f"final{piece}"):
            await_rows(gathered, 2, out_cuts[piece], own_sem.at[piece])
            total = kept[pl.ds(0, rows), low_col:high_col]
            total += got(0, 1, piece) + got(0, 2, piece)
        with jax.named_scope(f"end{piece}"):
            await_rows(gathered, 1, out_cuts[piece], back_sem.at[piece])
            total += from_far[:, low_col:high_col].astype(jnp.float32)
            high_col = min(high_col, width)
            out[:, low_col:high_col] = total[:, : high_col - low_col].astype(out.dtype)
    with jax.named_scope("drain_end"):
        await_sent(1)


GIVE_AT = None


def quad_local(tokens, routes, gate_fixed, gate_weight, up_weight, down_weight):
    rows, width = tokens.shape
    top = routes.shape[1]
    gate_weight = jnp.swapaxes(gate_weight, 1, 2)
    up_weight = jnp.swapaxes(up_weight, 1, 2)
    padded = -(-(width + 3 * top) // 128) * 128
    every = 16 * rows
    dma = pltpu.SemaphoreType.DMA
    ins, outs = dma((len(IN_SHARES),)), dma((len(OUT_SHARES),))
    anywhere = pl.BlockSpec(memory_space=pl.ANY)
    routes, gate_fixed = routes.T, gate_fixed.T
    return pl.pallas_call(
        quad_kernel,
        out_shape=pltpu.VMEM((rows, width), jnp.bfloat16),
        in_specs=[anywhere] * 6,
        out_specs=pl.BlockSpec(memory_space=pltpu.VMEM),
        scratch_shapes=[
            pltpu.VMEM(tokens.shape, jnp.bfloat16),
            pltpu.VMEM(routes.shape, jnp.int32),
            pltpu.VMEM(gate_fixed.shape, jnp.int32),
            pltpu.VMEM((every, padded), jnp.bfloat16),
            pltpu.VMEM(gate_weight.shape[1:], jnp.bfloat16),
            pltpu.VMEM(up_weight.shape[1:], jnp.bfloat16),
            pltpu.VMEM(down_weight.shape[1:], jnp.bfloat16),
            pltpu.VMEM((gate_weight.shape[1], every), jnp.float32),
            pltpu.VMEM((gate_weight.shape[1], every), jnp.float32),
            pltpu.VMEM((every, padded), jnp.bfloat16),
            pltpu.VMEM((8 * rows, padded), jnp.bfloat16),
            pltpu.VMEM((6 * rows, padded), jnp.bfloat16),
            pltpu.VMEM((6 * rows, padded), jnp.bfloat16),
            pltpu.VMEM((3 * rows, padded), jnp.float32),
            pltpu.VMEM((rows, padded), jnp.bfloat16),
            pltpu.VMEM((rows, padded), jnp.bfloat16),
            dma((3,)), dma((3,)), dma((2,)),
            ins, ins, ins, ins,
            outs, outs, outs, outs, outs,
        ],
        compiler_params=pltpu.CompilerParams(
            collective_id=0, has_side_effects=True, vmem_limit_bytes=60 * 2**20
        ),
    )(tokens, routes, gate_fixed, gate_weight, up_weight, down_weight)


def solution(mesh):
    placed = (
        P(("groups", "ep"), None),
        P(("groups", "ep"), None),
        P(("groups", "ep"), None),
        P("ep", None, None),
        P("ep", None, None),
        P("ep", None, None),
    )
    chips = mesh.shape["ep"] // 2

    def body(*args):
        if chips == 2**3:
            return quad_local(*args)
        return local(*args)

    return jax.shard_map(
        body, mesh=mesh, in_specs=placed, out_specs=P(("groups", "ep"), None), check_vma=False
    )
```

time: 35.4 us -> 31.9 us (0.901)
  Pallas kernels: 34.6 us -> 31.1 us
    pallas_call x1, Pallas kernels: 34.6 us -> 31.1 us  [quad_local(): pl.pallas_call(quad_kernel, out_shape=pltpu.VMEM((rows, width), jnp.bfloa...]
where the time goes in v2:
time: 31.9 us; the launch traced here: 31.8 us
  Pallas kernels  31.1 us (97%)
  local copies, waits for them, and re-layouts  0.64 us (2%)
    pallas_call x1, Pallas kernels, quad_local(): pl.pallas_call(quad_kernel, out_shape=pltpu.VMEM((rows, width), jnp.bfloa...  31.1 us
    unnamed x1, local copies, waits for them, and re-layouts  0.64 us

profile of v2, /device:TPU:0, one launch (start us, length us, event | category | flops | bytes accessed | tf_op | source)
XLA Modules:
  0.0 31.8 jit_solution(15565263068001297822)
XLA Ops:
  0.0 31.1 %shard_map.64 = bf16[16,2880]{1,0:T(8,128)(2,1)S(1)} custom-call(bf16[16,2880]{1,0:T(8,128)(2,1)} %tokens.1, s32[4,16]{1,0:T(4,128)} %bitcast.6, s32[4,16]{1,0:T(4,128)} %bitcast.7, bf16[1,720,2880]{2,1,0:T(8,128)(2,1)} %bitcast.4, bf16[1,720,2880]{2,1,0:T(8,128)(2,1)} %bitcast.5, bf16[1,720,2880]{2,1,0:T(8,128)(2,1)} %w_down.1), custom_call_target="tpu_custom_call" | custom-call | tf_op jit(solution)/shard_map/pallas_call | solution.py:367
  31.2 0.6 %copy.8 = bf16[16,2880]{1,0:T(8,128)(2,1)} copy(bf16[16,2880]{1,0:T(8,128)(2,1)S(1)} %shard_map.64) | data formatting | bytes 184320

commit v3 on v2

--- a/solution.py
+++ b/solution.py
@@ -78,16 +78,20 @@
 
 NT = (((1,), (1,)), ((), ()))
 TN = (((0,), (0,)), ((), ()))
-IN_SHARES = (8, 8, 7)
+IN_SHARES = (6, 6, 4, 7)
 OUT_SHARES = (8, 8, 7)
+GATHER = ("ZZZZ", "DDDD")
+SCATTER = ("XXX", "DDD")
+DIRECT = {"D": (1, 3, 2), "X": (1, 2), "Z": (2, 1)}
+VIA = {"X": 1, "Z": 2}
 
 
 def quad_kernel(
     tokens, routes, gates, w_gate, w_up, w_down, out,
     own_tokens, own_routes, own_gates, gathered, vm_gate, vm_up, vm_down, gate_sum, up_sum, partial,
-    from_core, to_quad, from_quad, kept, to_far, from_far,
-    in_sem, w_sem, sent, near_sem, far_sem, late_sem, core_sem,
-    pass_sem, quad_sem, side_sem, own_sem, back_sem,
+    from_core, to_quad, from_quad, to_far, from_far,
+    in_sem, w_sem, sent, near_sem, far_sem, mid_sem, late_sem, core_sem,
+    pass_sem, hop_sem, quad_sem, own_sem, back_sem,
 ):
     rows, width = own_tokens.shape
     top = own_routes.shape[0]
@@ -105,7 +109,7 @@
     diagonal = side_peer + pair_peer - device
     quad_peers = [None, side_peer, pair_peer, diagonal]
 
-    peers = [core_peer, side_peer, pair_peer, diagonal, far_peer]
+    peers = [core_peer, side_peer, pair_peer, far_peer]
     barrier = pltpu.get_barrier_semaphore()
     for peer in peers:
         pl.semaphore_signal(
@@ -129,6 +133,7 @@
     chunk_rows = 2 * block_rows
     edge = width // 128 * 128
     cuts = portions(padded, IN_SHARES)
+    cuts = cuts[-TURN:] + cuts[:-TURN]
     out_cuts = portions(padded, OUT_SHARES)
     pieces = range(len(cuts))
     out_pieces = range(len(out_cuts))
@@ -192,28 +197,51 @@
     def to_core(chunk, q, piece):
         give(slot(chunk, 0, q), chunk, 1, q, piece, core_sem, core_peer)
 
+    def spread(chunk, piece):
+        mode = GATHER[chunk][piece]
+        for q in DIRECT[mode]:
+            if chunk == 0 and q < 3:
+                recv_sem = near_sem
+            elif chunk == 1 and q == VIA.get(mode):
+                recv_sem = mid_sem
+            else:
+                recv_sem = late_sem
+            give(slot(chunk, 0, 0), chunk, 0, q, piece, recv_sem, quad_peers[q])
+        to_core(chunk, 0, piece)
+
+    def relay(chunk, piece):
+        mode = GATHER[chunk][piece]
+        if mode != "D":
+            q = VIA[mode]
+            give(slot(chunk, 0, q), chunk, 0, 3, piece, late_sem, quad_peers[3 - q])
+
     for piece in pieces:
         give(mine, 1, 0, 0, piece, far_sem, far_peer)
-        for q in (2, 1):
-            give(mine, 0, 0, q, piece, near_sem, quad_peers[q])
-        to_core(0, 0, piece)
+        spread(0, piece)
 
     def take_near(piece):
         await_rows(gathered, 2, cuts[piece], near_sem.at[piece])
-        give(slot(0, 0, 2), 0, 0, 3, piece, late_sem, side_peer)
+        relay(0, piece)
         for q in (2, 1):
             to_core(0, q, piece)
 
     def take_far(piece):
         await_rows(gathered, 1, cuts[piece], far_sem.at[piece])
-        for q in (3, 2, 1):
-            give(slot(1, 0, 0), 1, 0, q, piece, late_sem, quad_peers[q])
-        to_core(1, 0, piece)
+        spread(1, piece)
+
+    def take_mid(piece):
+        mode = GATHER[1][piece]
+        if mode != "D":
+            await_rows(gathered, 1, cuts[piece], mid_sem.at[piece])
+            relay(1, piece)
+            to_core(1, VIA[mode], piece)
 
     def take_late(piece):
-        await_rows(gathered, 4, cuts[piece], late_sem.at[piece])
+        mode = GATHER[1][piece]
+        rest = [q for q in (1, 2, 3) if q != VIA.get(mode)]
+        await_rows(gathered, 1 + len(rest), cuts[piece], late_sem.at[piece])
         to_core(0, 3, piece)
-        for q in (1, 2, 3):
+        for q in rest:
             to_core(1, q, piece)
 
     def add_products(piece):
@@ -234,19 +262,22 @@
             factor += jnp.where(info[:, col : col + 1] == expert, value, 0.0)
         return factor
 
-    def run_down(hidden, factor, piece):
+    def run_down(hidden, factor, chunk, piece):
         low_out, high_out = out_cuts[piece]
-        for low_col, high_col in column_cuts(low_out, min(high_out, width), 512):
+        low_row = chunk * chunk_rows
+        high_row = low_row + chunk_rows
+        for low_col, high_col in column_cuts(low_out, min(high_out, width), BLOCK):
             y = lax.dot_general(
-                hidden, vm_down[:, low_col:high_col], TN, preferred_element_type=jnp.float32
+                hidden[:, low_row:high_row], vm_down[:, low_col:high_col], TN,
+                preferred_element_type=jnp.float32,
             )
-            partial[:, low_col:high_col] = (y * factor).astype(jnp.bfloat16)
-        for chunk in (1, 0):
-            launch(
-                1, partial.at[pl.ds(chunk * chunk_rows + block_rows, block_rows), low_out:high_out],
-                from_core.at[pl.ds(chunk * block_rows, block_rows), low_out:high_out],
-                pass_sem.at[piece], core_peer,
-            )
+            part = (y * factor[low_row:high_row]).astype(jnp.bfloat16)
+            partial[low_row:high_row, low_col:high_col] = part
+        launch(
+            1, partial.at[pl.ds(low_row + block_rows, block_rows), low_out:high_out],
+            from_core.at[pl.ds(chunk * block_rows, block_rows), low_out:high_out],
+            pass_sem.at[chunk, piece], core_peer,
+        )
 
     def chip_sum(chunk, q, piece):
         low_col, high_col = out_cuts[piece]
@@ -267,80 +298,104 @@
         low_col, high_col = out_cuts[piece]
         return from_quad[pl.ds((chunk * 3 + q - 1) * rows, rows), low_col:high_col].astype(jnp.float32)
 
+    done_sem = (own_sem, quad_sem)
+
+    def give_out(chunk, q, piece):
+        mode = SCATTER[chunk][piece]
+        total = chip_sum(chunk, q, piece)
+        if q == 3 and mode != "D":
+            give_sum(total, chunk, 3, piece, hop_sem.at[chunk], quad_peers[VIA[mode]])
+        elif mode == "D" or q == VIA[mode]:
+            give_sum(total, chunk, q, piece, done_sem[chunk], quad_peers[q])
+
     def give_b(piece):
-        low_col, high_col = out_cuts[piece]
-        await_rows(gathered, 8, out_cuts[piece], pass_sem.at[piece])
+        await_rows(gathered, 4, out_cuts[piece], pass_sem.at[1, piece])
         for q in (3, 1, 2):
-            give_sum(chip_sum(1, q, piece), 1, q, piece, quad_sem, quad_peers[q])
-        kept[pl.ds(rows, rows), low_col:high_col] = chip_sum(1, 0, piece)
+            give_out(1, q, piece)
+
+    def relay_out(chunk, piece):
+        mode = SCATTER[chunk][piece]
+        if mode != "D":
+            q = 3 - VIA[mode]
+            await_rows(gathered, 1, out_cuts[piece], hop_sem.at[chunk, piece])
+            total = chip_sum(chunk, q, piece) + got(chunk, 3, piece)
+            give_sum(total, chunk, q, piece, done_sem[chunk], quad_peers[q])
+
+    def quad_total(chunk, piece):
+        direct = SCATTER[chunk][piece] == "D"
+        await_rows(gathered, 3 if direct else 2, out_cuts[piece], done_sem[chunk].at[piece])
+        total = chip_sum(chunk, 0, piece) + got(chunk, 1, piece) + got(chunk, 2, piece)
+        return total + got(chunk, 3, piece) if direct else total
 
     for piece in pieces:
         with jax.named_scope(f"near{piece}"):
             take_near(piece)
         with jax.named_scope(f"far{piece}"):
             take_far(piece)
+    for piece in pieces:
+        with jax.named_scope(f"mid{piece}"):
+            take_mid(piece)
     last = len(cuts) - 1
-    with jax.named_scope("late0"):
-        take_late(0)
-    weights[0].wait()
-    weights[1].wait()
-    for piece in pieces:
-        if piece < last:
-            with jax.named_scope(f"late{piece + 1}"):
-                take_late(piece + 1)
+    def dots(piece):
         with jax.named_scope(f"core{piece}"):
             await_rows(gathered, 8, cuts[piece], core_sem.at[piece])
         with jax.named_scope(f"dot{piece}"):
-            if piece == last:
-                factor = gate_factor()
             add_products(piece)
+
+    for piece in pieces:
+        with jax.named_scope(f"late{piece}"):
+            take_late(piece)
+        if piece == 0:
+            weights[0].wait()
+            weights[1].wait()
+        if piece > 0:
+            dots(piece - 1)
+    dots(last)
+    factor = gate_factor()
     with jax.named_scope("silu"):
         hidden = (jax.nn.silu(gate_sum[...]) * up_sum[...]).astype(jnp.bfloat16)
     weights[2].wait()
+    with jax.named_scope("down1"):
+        for piece in out_pieces:
+            run_down(hidden, factor, 1, piece)
+    gave = 0
     for piece in out_pieces:
-        with jax.named_scope(f"down{piece}"):
-            run_down(hidden, factor, piece)
-        if piece == GIVE_AT:
-            with jax.named_scope("give1_0"):
-                give_b(0)
-    with jax.named_scope("give1"):
-        for piece in out_pieces:
-            if piece > 0 or GIVE_AT is None:
-                give_b(piece)
+        with jax.named_scope(f"down0_{piece}"):
+            run_down(hidden, factor, 0, piece)
+        if piece >= GIVE_AT:
+            with jax.named_scope(f"give1_{gave}"):
+                give_b(gave)
+            gave += 1
+    for piece in list(out_pieces)[gave:]:
+        with jax.named_scope(f"give1_{piece}"):
+            give_b(piece)
+    for piece in out_pieces:
+        await_rows(gathered, 4, out_cuts[piece], pass_sem.at[0, piece])
     with jax.named_scope("give0"):
-        for q, recv_sem in ((3, side_sem), (1, own_sem)):
+        for q in (3, 1):
             for piece in out_pieces:
-                give_sum(chip_sum(0, q, piece), 0, q, piece, recv_sem, side_peer)
-    with jax.named_scope("kept"):
-        for piece in out_pieces:
-            low_col, high_col = out_cuts[piece]
-            kept[pl.ds(0, rows), low_col:high_col] = chip_sum(0, 0, piece)
-            kept[pl.ds(2 * rows, rows), low_col:high_col] = chip_sum(0, 2, piece)
-    for piece in out_pieces:
+                give_out(0, q, piece)
+
+    def far_out(piece):
         low_col, high_col = out_cuts[piece]
-        with jax.named_scope(f"far_out{piece}"):
-            await_rows(gathered, 3, out_cuts[piece], quad_sem.at[piece])
-            total = kept[pl.ds(rows, rows), low_col:high_col]
-            total += got(1, 1, piece) + got(1, 2, piece) + got(1, 3, piece)
-            to_far[:, low_col:high_col] = total.astype(jnp.bfloat16)
-            launch(
-                1, to_far.at[:, low_col:high_col], from_far.at[:, low_col:high_col],
-                back_sem.at[piece], far_peer,
-            )
-    for piece in out_pieces:
-        low_col, high_col = out_cuts[piece]
-        with jax.named_scope(f"relay{piece}"):
-            await_rows(gathered, 1, out_cuts[piece], side_sem.at[piece])
-            total = kept[pl.ds(2 * rows, rows), low_col:high_col] + got(0, 3, piece)
-            give_sum(total, 0, 2, piece, own_sem, pair_peer)
+        to_far[:, low_col:high_col] = quad_total(1, piece).astype(jnp.bfloat16)
+        launch(
+            1, to_far.at[:, low_col:high_col], from_far.at[:, low_col:high_col],
+            back_sem.at[piece], far_peer,
+        )
+
+    for kind, piece in PLAN:
+        with jax.named_scope(f"{kind}{piece}"):
+            if kind == "hop":
+                relay_out(0, piece)
+            else:
+                far_out(piece)
     with jax.named_scope("drain"):
         await_sent(0)
     for piece in out_pieces:
         low_col, high_col = out_cuts[piece]
         with jax.named_scope(f"final{piece}"):
-            await_rows(gathered, 2, out_cuts[piece], own_sem.at[piece])
-            total = kept[pl.ds(0, rows), low_col:high_col]
-            total += got(0, 1, piece) + got(0, 2, piece)
+            total = quad_total(0, piece)
         with jax.named_scope(f"end{piece}"):
             await_rows(gathered, 1, out_cuts[piece], back_sem.at[piece])
             total += from_far[:, low_col:high_col].astype(jnp.float32)
@@ -350,7 +405,10 @@
         await_sent(1)
 
 
-GIVE_AT = None
+GIVE_AT = 0
+PLAN = (("far", 0), ("far", 1), ("hop", 0), ("far", 2), ("hop", 1), ("hop", 2))
+TURN = 1
+BLOCK = 1024
 
 
 def quad_local(tokens, routes, gate_fixed, gate_weight, up_weight, down_weight):
@@ -383,12 +441,11 @@
             pltpu.VMEM((8 * rows, padded), jnp.bfloat16),
             pltpu.VMEM((6 * rows, padded), jnp.bfloat16),
             pltpu.VMEM((6 * rows, padded), jnp.bfloat16),
-            pltpu.VMEM((3 * rows, padded), jnp.float32),
             pltpu.VMEM((rows, padded), jnp.bfloat16),
             pltpu.VMEM((rows, padded), jnp.bfloat16),
             dma((3,)), dma((3,)), dma((2,)),
-            ins, ins, ins, ins,
-            outs, outs, outs, outs, outs,
+            ins, ins, ins, ins, ins,
+            dma((2, len(OUT_SHARES))), dma((2, len(OUT_SHARES))), outs, outs, outs,
         ],
         compiler_params=pltpu.CompilerParams(
             collective_id=0, has_side_effects=True, vmem_limit_bytes=60 * 2**20

time: 31.9 us -> 31.3 us (0.981)
  Pallas kernels: 31.1 us -> 30.5 us
    pallas_call x1, Pallas kernels: 31.1 us -> 30.5 us  [quad_local(): pl.pallas_call(quad_kernel, out_shape=pltpu.VMEM((rows, width), jnp.bfloa...]
where the time goes in v3:
time: 31.3 us; the launch traced here: 31.1 us
  Pallas kernels  30.5 us (97%)
  local copies, waits for them, and re-layouts  0.64 us (2%)
    pallas_call x1, Pallas kernels, quad_local(): pl.pallas_call(quad_kernel, out_shape=pltpu.VMEM((rows, width), jnp.bfloa...  30.5 us
    unnamed x1, local copies, waits for them, and re-layouts  0.64 us

profile of v3, /device:TPU:0, one launch (start us, length us, event | category | flops | bytes accessed | tf_op | source)
XLA Modules:
  0.0 31.1 jit_solution(16819777467697115590)
XLA Ops:
  0.0 30.5 %shard_map.64 = bf16[16,2880]{1,0:T(8,128)(2,1)S(1)} custom-call(bf16[16,2880]{1,0:T(8,128)(2,1)} %tokens.1, s32[4,16]{1,0:T(4,128)} %bitcast.6, s32[4,16]{1,0:T(4,128)} %bitcast.7, bf16[1,720,2880]{2,1,0:T(8,128)(2,1)} %bitcast.4, bf16[1,720,2880]{2,1,0:T(8,128)(2,1)} %bitcast.5, bf16[1,720,2880]{2,1,0:T(8,128)(2,1)} %w_down.1), custom_call_target="tpu_custom_call" | custom-call | tf_op jit(solution)/shard_map/pallas_call | solution.py:425
  30.5 0.6 %copy.8 = bf16[16,2880]{1,0:T(8,128)(2,1)} copy(bf16[16,2880]{1,0:T(8,128)(2,1)S(1)} %shard_map.64) | data formatting | bytes 184320

commit v4 on v3

--- a/solution.py
+++ b/solution.py
@@ -80,7 +80,7 @@
 TN = (((0,), (0,)), ((), ()))
 IN_SHARES = (6, 6, 4, 7)
 OUT_SHARES = (8, 8, 7)
-GATHER = ("ZZZZ", "DDDD")
+GATHER = ("ZZXZ", "DDDD")
 SCATTER = ("XXX", "DDD")
 DIRECT = {"D": (1, 3, 2), "X": (1, 2), "Z": (2, 1)}
 VIA = {"X": 1, "Z": 2}
@@ -342,16 +342,18 @@
         with jax.named_scope(f"dot{piece}"):
             add_products(piece)
 
-    for piece in pieces:
-        with jax.named_scope(f"late{piece}"):
-            take_late(piece)
+    for kind, piece in STEPS:
+        if kind == "late":
+            with jax.named_scope(f"late{piece}"):
+                take_late(piece)
+            continue
         if piece == 0:
             weights[0].wait()
             weights[1].wait()
-        if piece > 0:
-            dots(piece - 1)
-    dots(last)
-    factor = gate_factor()
+        if piece == FACTOR:
+            with jax.named_scope("factor"):
+                factor = gate_factor()
+        dots(piece)
     with jax.named_scope("silu"):
         hidden = (jax.nn.silu(gate_sum[...]) * up_sum[...]).astype(jnp.bfloat16)
     weights[2].wait()
@@ -388,6 +390,8 @@
         with jax.named_scope(f"{kind}{piece}"):
             if kind == "hop":
                 relay_out(0, piece)
+            elif kind == "pair":
+                give_out(0, 2, piece)
             else:
                 far_out(piece)
     with jax.named_scope("drain"):
@@ -409,6 +413,8 @@
 PLAN = (("far", 0), ("far", 1), ("hop", 0), ("far", 2), ("hop", 1), ("hop", 2))
 TURN = 1
 BLOCK = 1024
+FACTOR = 2
+STEPS = [("late", 0), ("late", 1), ("dot", 0), ("late", 2), ("late", 3), ("dot", 1), ("dot", 2), ("dot", 3)]
 
 
 def quad_local(tokens, routes, gate_fixed, gate_weight, up_weight, down_weight):

time: 31.3 us -> 31.1 us (level)
  no operation moved by 1% of the time
where the time goes in v4:
time: 31.1 us; the launch traced here: 31 us
  Pallas kernels  30.3 us (97%)
  local copies, waits for them, and re-layouts  0.64 us (2%)
    pallas_call x1, Pallas kernels, quad_local(): pl.pallas_call(quad_kernel, out_shape=pltpu.VMEM((rows, width), jnp.bfloa...  30.3 us
    unnamed x1, local copies, waits for them, and re-layouts  0.64 us

profile of v4, /device:TPU:0, one launch (start us, length us, event | category | flops | bytes accessed | tf_op | source)
XLA Modules:
  0.0 31.0 jit_solution(14457861616370824243)
XLA Ops:
  0.0 30.3 %shard_map.64 = bf16[16,2880]{1,0:T(8,128)(2,1)S(1)} custom-call(bf16[16,2880]{1,0:T(8,128)(2,1)} %tokens.1, s32[4,16]{1,0:T(4,128)} %bitcast.6, s32[4,16]{1,0:T(4,128)} %bitcast.7, bf16[1,720,2880]{2,1,0:T(8,128)(2,1)} %bitcast.4, bf16[1,720,2880]{2,1,0:T(8,128)(2,1)} %bitcast.5, bf16[1,720,2880]{2,1,0:T(8,128)(2,1)} %w_down.1), custom_call_target="tpu_custom_call" | custom-call | tf_op jit(solution)/shard_map/pallas_call | solution.py:431
  30.3 0.6 %copy.8 = bf16[16,2880]{1,0:T(8,128)(2,1)} copy(bf16[16,2880]{1,0:T(8,128)(2,1)S(1)} %shard_map.64) | data formatting | bytes 184320

commit v5 on v4

--- a/solution.py
+++ b/solution.py
@@ -253,6 +253,21 @@
             )
             total[...] = product if piece == 0 else total[...] + product
 
+    def finish_hidden(piece):
+        low_col, high_col = cuts[piece][0], min(cuts[piece][1], width)
+        x = gathered[:, low_col:high_col]
+        parts = []
+        for low_row, high_row in column_cuts(0, vm_gate.shape[0], ROWS):
+            g, u = (
+                total[low_row:high_row, :] + lax.dot_general(
+                    weight[low_row:high_row, low_col:high_col], x, NT,
+                    preferred_element_type=jnp.float32,
+                )
+                for weight, total in ((vm_gate, gate_sum), (vm_up, up_sum))
+            )
+            parts.append((jax.nn.silu(g) * u).astype(jnp.bfloat16))
+        return jnp.concatenate(parts, axis=0)
+
     def gate_factor():
         info = gathered[:, edge:].astype(jnp.float32)
         factor = jnp.zeros((2 * chunk_rows, 1), jnp.float32)
@@ -353,9 +368,12 @@
         if piece == FACTOR:
             with jax.named_scope("factor"):
                 factor = gate_factor()
-        dots(piece)
-    with jax.named_scope("silu"):
-        hidden = (jax.nn.silu(gate_sum[...]) * up_sum[...]).astype(jnp.bfloat16)
+        if piece < last:
+            dots(piece)
+    with jax.named_scope(f"core{last}"):
+        await_rows(gathered, 8, cuts[last], core_sem.at[last])
+    with jax.named_scope("hidden"):
+        hidden = finish_hidden(last)
     weights[2].wait()
     with jax.named_scope("down1"):
         for piece in out_pieces:
@@ -414,6 +432,7 @@
 TURN = 1
 BLOCK = 1024
 FACTOR = 2
+ROWS = 240
 STEPS = [("late", 0), ("late", 1), ("dot", 0), ("late", 2), ("late", 3), ("dot", 1), ("dot", 2), ("dot", 3)]
 
 
@@ -450,8 +469,8 @@
             pltpu.VMEM((rows, padded), jnp.bfloat16),
             pltpu.VMEM((rows, padded), jnp.bfloat16),
             dma((3,)), dma((3,)), dma((2,)),
-            ins, ins, ins, ins, ins,
-            dma((2, len(OUT_SHARES))), dma((2, len(OUT_SHARES))), outs, outs, outs,
+            ins, ins, dma((1,)), ins, ins,
+            dma((2, len(OUT_SHARES))), dma((1, len(OUT_SHARES))), outs, outs, outs,
         ],
         compiler_params=pltpu.CompilerParams(
             collective_id=0, has_side_effects=True, vmem_limit_bytes=60 * 2**20

time: 31.1 us -> 31.1 us (level)
  no operation moved by 1% of the time
where the time goes in v5:
time: 31.1 us; the launch traced here: 30.9 us
  Pallas kernels  30.3 us (97%)
  local copies, waits for them, and re-layouts  0.64 us (2%)
    pallas_call x1, Pallas kernels, quad_local(): pl.pallas_call(quad_kernel, out_shape=pltpu.VMEM((rows, width), jnp.bfloa...  30.3 us
    unnamed x1, local copies, waits for them, and re-layouts  0.64 us

profile of v5, /device:TPU:0, one launch (start us, length us, event | category | flops | bytes accessed | tf_op | source)
XLA Modules:
  0.0 30.9 jit_solution(13918152538406964325)
XLA Ops:
  0.0 30.3 %shard_map.64 = bf16[16,2880]{1,0:T(8,128)(2,1)S(1)} custom-call(bf16[16,2880]{1,0:T(8,128)(2,1)} %tokens.1, s32[4,16]{1,0:T(4,128)} %bitcast.6, s32[4,16]{1,0:T(4,128)} %bitcast.7, bf16[1,720,2880]{2,1,0:T(8,128)(2,1)} %bitcast.4, bf16[1,720,2880]{2,1,0:T(8,128)(2,1)} %bitcast.5, bf16[1,720,2880]{2,1,0:T(8,128)(2,1)} %w_down.1), custom_call_target="tpu_custom_call" | custom-call | tf_op jit(solution)/shard_map/pallas_call | solution.py:450
  30.3 0.6 %copy.8 = bf16[16,2880]{1,0:T(8,128)(2,1)} copy(bf16[16,2880]{1,0:T(8,128)(2,1)S(1)} %shard_map.64) | data formatting | bytes 184320
